TPU v7x, 32 devices: a whole 2x2x4 slice. The times are simulated.
32 devices in a mesh: row: 8 (over z, x), col: 4 (over y, core).
Axes of the slice: x: 2, y: 2, z: 4, core: 2. Of those that a mesh axis runs over, the one named last changes fastest.
Arguments:
- forward_map: float32 [2048, 16384], P('row', 'col'), may hold values from -0.125 to 0.125
- sensor_weights: float32 [2048], P('row'), may hold values from 0.25 to 4
- sensor_mask: int32 [2048], P('row'), may hold values 0 or 1
Outputs:
- gram_matrix: float32 [16384, 16384], P('row', 'col')
All inputs are finite; a program needn't handle non-finite values. No bound on the sum of `sensor_mask` on one device may be relied on, other than what follows from the above.
Results may differ from a plain program's by a relative error of at most 0.000061.
Values sent between devices are 32-bit elements; how exact they have to be, the bound alone decides.
No kernel may reach another device: no remote copies, remote signals or barrier semaphores. Data moves between devices by JAX's collectives and lax.ppermute only.
A program may use at most 128 MiB of HBM per device.

v0:
```python
import jax
import jax.numpy as jnp
from jax import lax
from jax.sharding import PartitionSpec as P


def contract(left_rows, right_rows):
    return lax.dot_general(
        left_rows,
        right_rows,
        (((0,), (0,)), ((), ())),
        precision=lax.Precision.HIGHEST,
        preferred_element_type=jnp.float32,
    )


def per_device(forward_map, sensor_weights, sensor_mask):
    sensor_scale = sensor_weights * sensor_mask.astype(jnp.float32)
    weighted = forward_map * sensor_scale[:, None]
    gathered = lax.all_gather(weighted, "row", axis=0, tiled=True)
    spread = lax.all_to_all(forward_map, "col", split_axis=0, concat_axis=1, tiled=True)
    regrouped = lax.all_to_all(spread, "row", split_axis=1, concat_axis=0, tiled=True)
    rows_count = lax.axis_size("row")
    cols_count = lax.axis_size("col")
    columns = gathered.shape[1]
    stride_rows = gathered.shape[0] // (rows_count * cols_count)
    permuted = (
        gathered.reshape(rows_count, cols_count, stride_rows, columns)
        .transpose(1, 0, 2, 3)
        .reshape(-1, columns)
    )
    return contract(lax.all_gather(regrouped, "col", axis=0, tiled=True), permuted)


def solution(mesh):
    placed = (P("row", "col"), P("row"), P("row"))
    return jax.shard_map(
        per_device, mesh=mesh, in_specs=placed, out_specs=P("row", "col"), check_vma=False
    )
```

profile of v0, /device:TPU:0, one launch (start us, length us, event | category | flops | bytes accessed | tf_op | source)
XLA Modules:
  0.0 1065.3 jit_solution(8509121159541855739)
XLA Ops:
  6.5 0.0 all-gather.3.cloned.1.call-start
  6.5 0.7 convert_multiply_fusion
  7.2 4.8 broadcast_multiply_fusion
  12.0 0.0 all-gather.3.cloned.1.call-update
  12.0 0.0 all-gather.5.cloned.1.call-start
  12.1 52.6 %all_to_all.35 = f32[4,64,4096]{2,1,0:T(8,128)S(1)} all-to-all(f32[4,64,4096]{2,1,0:T(8,128)} %bitcast.15), channel_id=1, replica_groups=mesh['row'=8,'col'=4] {'col'}, dimensions={0} | all-to-all | bytes 8388608 | tf_op jit(solution)/shard_map/all_to_all | solution.py:21
  64.7 4.7 copy.13
  69.4 5.5 all_to_all.29
  74.9 4.6 copy.14
  79.5 136.9 %all_to_all.36 = f32[64,8,2048]{2,0,1:T(8,128)} all-to-all(f32[64,8,2048]{2,0,1:T(8,128)S(1)} %copy.14), channel_id=1, replica_groups=mesh['row'=8,'col'=4] {'row'}, dimensions={1} | all-to-all | bytes 8388608 | tf_op jit(solution)/shard_map/all_to_all | solution.py:22
  216.4 0.0 all-gather.5.cloned.1.call-update
  216.4 481.1 %all-gather.3.cloned.1.call-done = f32[2048,4096]{1,0:T(8,128)} async-done(((f32[256,4096]{1,0:T(8,128)}), f32[2048,4096]{1,0:T(8,128)}) %all-gather.3.cloned.1.call-update) | async-done | bytes 33554448 | tf_op jit(solution)/shard_map/all_gather | solution.py:20
  697.5 24.4 %copy.12 = f32[4,8,64,4096]{3,2,1,0:T(8,128)} copy(f32[4,8,64,4096]{3,2,0,1:T(8,128)} %bitcast.13) | data formatting | bytes 67108864 | tf_op jit(solution)/shard_map/transpose | solution.py:29
  721.9 83.1 %all-gather.5.cloned.1.call-done = f32[2048,2048]{1,0:T(8,128)} async-done(((f32[512,2048]{1,0:T(8,128)}), f32[2048,2048]{1,0:T(8,128)}) %all-gather.5.cloned.1.call-update) | async-done | bytes 16777232 | tf_op jit(solution)/shard_map/all_gather | solution.py:32
  805.0 222.4 %convolution_bitcast_fusion = f32[2048,4096]{0,1:T(8,128)} fusion(f32[2048,4096]{1,0:T(8,128)} %bitcast.14, f32[2048,2048]{1,0:T(8,128)} %all-gather.5.cloned.1.call-done), kind=kOutput, calls=%fused_computation | convolution fusion | flops 206158430208 | bytes 83886080 | tf_op jit(solution)/shard_map/dot_general | solution.py:8
  1027.4 31.1 %copy.15 = f32[2048,4096]{1,0:T(8,128)} copy(f32[2048,4096]{0,1:T(8,128)} %convolution_bitcast_fusion) | data formatting | bytes 67108864 | tf_op jit(solution)/shard_map/dot_general | solution.py:8
Async XLA Ops:
  6.5 691.0 %all-gather.3.cloned.1.call-start = ((), (), s32[]{:S(2)}) async-start(), calls=%async_computation.2 | async-start | bytes 37748736 | tf_op jit(solution)/shard_map/all_gather | solution.py:20
  12.0 792.9 %all-gather.5.cloned.1.call-start = ((), (), s32[]{:S(2)}) async-start(), calls=%async_computation.3 | async-start | bytes 20971520 | tf_op jit(solution)/shard_map/all_gather | solution.py:32
Sparse Core Ops, SparseCore 0:
  12.2 685.3 all-gather.2
  699.1 105.8 all-gather.4
where the time goes:
time: 1070 us
  waiting for transfers between devices  564 us (53%)
  matrix products  222 us (21%)
  blocking collectives  189 us (18%)
  local copies, waits for them, and re-layouts  70.2 us (7%)
  between operations  13.4 us (1%)
    all_gather x1, waiting for transfers between devices, per_device(): gathered = lax.all_gather(weighted, 'row', axis=0, tiled=True)  481 us
    dot_general x1, matrix products, contract(): lax.dot_general(left_rows, right_rows, (((0,), (0,)), ((), ())), precisio...  222 us
    all_to_all x1, blocking collectives, per_device(): lax.all_to_all(spread, 'row', split_axis=1, concat_axis=0, tiled=True)  137 us
    all_gather x1, waiting for transfers between devices, per_device(): lax.all_gather(regrouped, 'col', axis=0, tiled=True)  83.1 us
    all_to_all x1, blocking collectives, per_device(): lax.all_to_all(forward_map, 'col', split_axis=0, concat_axis=1, tiled=True)  52.6 us
    dot_general x1, local copies, waits for them, and re-layouts, contract(): lax.dot_general(left_rows, right_rows, (((0,), (0,)), ((), ())), precisio...  31.1 us
    transpose x1, local copies, waits for them, and re-layouts, per_device(): permuted = gathered.reshape(rows_count, cols_count, stride_rows, columns)...  24.4 us
  transfers between devices with their start and end apart: 2, of which 2 were waited for; matrix products, arithmetic and copies ran while one was open for 3% of the time, Pallas kernels for 0%

commit v1 on v0

--- a/solution.py
+++ b/solution.py
@@ -2,6 +2,19 @@
 import jax.numpy as jnp
 from jax import lax
 from jax.sharding import PartitionSpec as P
+from jax.lax import all_to_all, psum
+
+
+def get_stages_all_on(view, dev_axis, which_dim, in_dim):
+    return jnp.concatenate(
+        all_to_all(
+            jnp.stack(jnp.split(view, psum(1, axis_name=dev_axis), which_dim)),
+            axis_name=dev_axis,
+            split_axis=0,
+            concat_axis=0,
+        ),
+        in_dim,
+    )
 
 
 def contract(left_rows, right_rows):
@@ -19,7 +32,7 @@
     weighted = forward_map * sensor_scale[:, None]
     gathered = lax.all_gather(weighted, "row", axis=0, tiled=True)
     spread = lax.all_to_all(forward_map, "col", split_axis=0, concat_axis=1, tiled=True)
-    regrouped = lax.all_to_all(spread, "row", split_axis=1, concat_axis=0, tiled=True)
+    regrouped = get_stages_all_on(spread, "row", 1, 0)
     rows_count = lax.axis_size("row")
     cols_count = lax.axis_size("col")
     columns = gathered.shape[1]

time: 1070 us -> 1030 us (0.963)
  local copies, waits for them, and re-layouts: 70.2 us -> 24.9 us
    dot_general x1 -> x0, local copies, waits for them, and re-layouts: 31.1 us -> none  [contract(): lax.dot_general(left_rows, right_rows, (((0,), (0,)), ((), ())), precisio...]
  transfers between devices with their start and end apart: 2 -> 2, of which waited for: 2 -> 2; matrix products, arithmetic and copies ran while one was open for 3% -> 2% of each run, Pallas kernels for 0% -> 0%
where the time goes in v1:
time: 1030 us
  waiting for transfers between devices  571 us (55%)
  matrix products  222 us (22%)
  blocking collectives  197 us (19%)
  local copies, waits for them, and re-layouts  24.9 us (2%)
  between operations  13.5 us (1%)
    all_gather x1, waiting for transfers between devices, per_device(): gathered = lax.all_gather(weighted, 'row', axis=0, tiled=True)  488 us
    dot_general x1, matrix products, contract(): lax.dot_general(left_rows, right_rows, (((0,), (0,)), ((), ())), precisio...  222 us
    all_to_all x1, blocking collectives, get_stages_all_on(): all_to_all(jnp.stack(jnp.split(view, psum(1, axis_name=dev_axis), which_d...  144 us
    all_gather x1, waiting for transfers between devices, per_device(): lax.all_gather(regrouped, 'col', axis=0, tiled=True)  83.3 us
    all_to_all x1, blocking collectives, per_device(): lax.all_to_all(forward_map, 'col', split_axis=0, concat_axis=1, tiled=True)  52.6 us
    transpose x1, local copies, waits for them, and re-layouts, per_device(): permuted = gathered.reshape(rows_count, cols_count, stride_rows, columns)...  24.2 us
  transfers between devices with their start and end apart: 2, of which 2 were waited for; matrix products, arithmetic and copies ran while one was open for 2% of the time, Pallas kernels for 0%

profile of v1, /device:TPU:0, one launch (start us, length us, event | category | flops | bytes accessed | tf_op | source)
XLA Modules:
  0.0 1034.2 jit_solution(4547697736424987361)
XLA Ops:
  6.5 0.0 all-gather.5.cloned.1.call-start
  6.5 0.7 convert_multiply_fusion
  7.2 4.8 broadcast_multiply_fusion
  12.0 0.0 all-gather.5.cloned.1.call-update
  12.0 0.0 all-gather.3.cloned.1.call-start
  12.1 52.6 %all_to_all.24 = f32[4,64,4096]{2,1,0:T(8,128)S(1)} all-to-all(f32[4,64,4096]{2,1,0:T(8,128)} %bitcast.53), channel_id=1, replica_groups=mesh['row'=8,'col'=4] {'col'}, dimensions={0} | all-to-all | bytes 8388608 | tf_op jit(solution)/shard_map/all_to_all | solution.py:34
  64.7 0.4 copy.9
  65.5 144.5 %all_to_all.25 = f32[8,64,2048]{2,1,0:T(8,128)} all-to-all(f32[8,64,2048]{2,1,0:T(8,128)S(1)} %fusion), channel_id=1, replica_groups=mesh['row'=8,'col'=4] {'row'}, dimensions={0} | all-to-all | bytes 8388608 | tf_op jit(solution)/shard_map/all_to_all | solution.py:10
  210.0 0.0 all-gather.3.cloned.1.call-update
  210.0 487.5 %all-gather.5.cloned.1.call-done = f32[2048,4096]{1,0:T(8,128)} async-done(((f32[256,4096]{1,0:T(8,128)}), f32[2048,4096]{1,0:T(8,128)}) %all-gather.5.cloned.1.call-update) | async-done | bytes 33554448 | tf_op jit(solution)/shard_map/all_gather | solution.py:33
  697.5 24.2 %copy.8 = f32[4,8,64,4096]{3,2,1,0:T(8,128)} copy(f32[4,8,64,4096]{3,2,0,1:T(8,128)} %bitcast.43) | data formatting | bytes 67108864 | tf_op jit(solution)/shard_map/transpose | solution.py:42
  721.7 83.3 %all-gather.3.cloned.1.call-done = f32[2048,2048]{1,0:T(8,128)} async-done(((f32[512,2048]{1,0:T(8,128)}), f32[2048,2048]{1,0:T(8,128)}) %all-gather.3.cloned.1.call-update) | async-done | bytes 16777232 | tf_op jit(solution)/shard_map/all_gather | solution.py:45
  805.0 222.3 %fusion.8 = f32[2048,4096]{1,0:T(8,128)} fusion(f32[2048,2048]{1,0:T(8,128)} %all-gather.3.cloned.1.call-done, f32[2048,4096]{1,0:T(8,128)} %bitcast.44), kind=kOutput, calls=%fused_computation.18 | convolution fusion | flops 206158430208 | bytes 83886080 | tf_op jit(solution)/shard_map/dot_general | solution.py:21
  (8 shorter events, 0.3 us)
Async XLA Ops:
  6.5 691.0 %all-gather.5.cloned.1.call-start = ((), (), s32[]{:S(2)}) async-start(), calls=%async_computation.3 | async-start | bytes 37748736 | tf_op jit(solution)/shard_map/all_gather | solution.py:33
  12.0 792.9 %all-gather.3.cloned.1.call-start = ((), (), s32[]{:S(2)}) async-start(), calls=%async_computation.2 | async-start | bytes 20971520 | tf_op jit(solution)/shard_map/all_gather | solution.py:45
Sparse Core Ops, SparseCore 0:
  12.2 685.3 all-gather.4
  699.1 105.8 all-gather.2

commit v2 on v0

--- a/solution.py
+++ b/solution.py
@@ -2,6 +2,11 @@
 import jax.numpy as jnp
 from jax import lax
 from jax.sharding import PartitionSpec as P
+
+
+def gather_over(array, name, d):
+    stack = jnp.stack([array] * lax.axis_size(name))
+    return jnp.concatenate(lax.all_to_all(stack, name, 0, 0), axis=d)
 
 
 def contract(left_rows, right_rows):
@@ -29,7 +34,7 @@
         .transpose(1, 0, 2, 3)
         .reshape(-1, columns)
     )
-    return contract(lax.all_gather(regrouped, "col", axis=0, tiled=True), permuted)
+    return contract(gather_over(regrouped, "col", 0), permuted)
 
 
 def solution(mesh):

time: 1070 us -> 982 us (0.918)
  waiting for transfers between devices: 564 us -> 466 us
    all_gather x1 -> x0, waiting for transfers between devices: 83.1 us -> none  [per_device(): lax.all_gather(regrouped, 'col', axis=0, tiled=True)]
    all_gather x1, waiting for transfers between devices: 481 us -> 466 us  [per_device(): gathered = lax.all_gather(weighted, 'row', axis=0, tiled=True)]
  transfers between devices with their start and end apart: 2 -> 2, of which waited for: 2 -> 1; matrix products, arithmetic and copies ran while one was open for 3% -> 4% of each run, Pallas kernels for 0% -> 0%
where the time goes in v2:
time: 982 us; the launch traced here: 981 us
  waiting for transfers between devices  466 us (47%)
  matrix products  222 us (23%)
  blocking collectives  189 us (19%)
  local copies, waits for them, and re-layouts  77.3 us (8%)
  between operations  13.4 us (1%)
    all_gather x1, waiting for transfers between devices, per_device(): gathered = lax.all_gather(weighted, 'row', axis=0, tiled=True)  466 us
    dot_general x1, matrix products, contract(): lax.dot_general(left_rows, right_rows, (((0,), (0,)), ((), ())), precisio...  222 us
    all_to_all x1, blocking collectives, per_device(): lax.all_to_all(spread, 'row', split_axis=1, concat_axis=0, tiled=True)  137 us
    all_to_all x1, blocking collectives, per_device(): lax.all_to_all(forward_map, 'col', split_axis=0, concat_axis=1, tiled=True)  52.6 us
    dot_general x1, local copies, waits for them, and re-layouts, contract(): lax.dot_general(left_rows, right_rows, (((0,), (0,)), ((), ())), precisio...  31.1 us
    transpose x1, local copies, waits for them, and re-layouts, per_device(): permuted = gathered.reshape(rows_count, cols_count, stride_rows, columns)...  23.1 us
  transfers between devices with their start and end apart: 2, of which 1 were waited for; matrix products, arithmetic and copies ran while one was open for 4% of the time, Pallas kernels for 0%

profile of v2, /device:TPU:0, one launch (start us, length us, event | category | flops | bytes accessed | tf_op | source)
XLA Modules:
  0.0 980.9 jit_solution(14842906037720717389)
XLA Ops:
  6.5 0.0 all-gather.2.cloned.1.call-start
  6.5 0.7 convert_multiply_fusion
  7.2 4.8 broadcast_multiply_fusion
  12.0 0.0 all-gather.2.cloned.1.call-update
  12.0 52.6 %all_to_all.37 = f32[4,64,4096]{2,1,0:T(8,128)S(1)} all-to-all(f32[4,64,4096]{2,1,0:T(8,128)} %bitcast.17), channel_id=1, replica_groups=mesh['row'=8,'col'=4] {'col'}, dimensions={0} | all-to-all | bytes 8388608 | tf_op jit(solution)/shard_map/all_to_all | solution.py:26
  64.7 4.8 copy.13
  69.4 5.5 all_to_all.30
  74.9 4.6 copy.14
  79.5 136.8 %all_to_all.38 = f32[64,8,2048]{2,0,1:T(8,128)S(1)} all-to-all(f32[64,8,2048]{2,0,1:T(8,128)S(1)} %copy.14), channel_id=1, replica_groups=mesh['row'=8,'col'=4] {'row'}, dimensions={1} | all-to-all | bytes 8388608 | tf_op jit(solution)/shard_map/all_to_all | solution.py:27
  216.3 8.3 stack.10
  224.6 7.3 all-to-all-start.2
  231.9 465.6 %all-gather.2.cloned.1.call-done = f32[2048,4096]{1,0:T(8,128)} async-done(((f32[256,4096]{1,0:T(8,128)}), f32[2048,4096]{1,0:T(8,128)}) %all-gather.2.cloned.1.call-update) | async-done | bytes 33554448 | tf_op jit(solution)/shard_map/all_gather | solution.py:25
  697.5 23.1 %copy.12 = f32[4,8,64,4096]{3,2,1,0:T(8,128)} copy(f32[4,8,64,4096]{3,2,0,1:T(8,128)} %bitcast.14) | data formatting | bytes 67108864 | tf_op jit(solution)/shard_map/transpose | solution.py:34
  720.6 0.0 all-to-all-done.2
  720.6 222.4 %convolution_bitcast_fusion = f32[2048,4096]{0,1:T(8,128)} fusion(f32[2048,4096]{1,0:T(8,128)} %bitcast.15, f32[2048,2048]{1,0:T(8,128)} %bitcast.7), kind=kOutput, calls=%fused_computation | convolution fusion | flops 206158430208 | bytes 83886080 | tf_op jit(solution)/shard_map/dot_general | solution.py:13
  943.0 31.1 %copy.15 = f32[2048,4096]{1,0:T(8,128)} copy(f32[2048,4096]{0,1:T(8,128)} %convolution_bitcast_fusion) | data formatting | bytes 67108864 | tf_op jit(solution)/shard_map/dot_general | solution.py:13
Async XLA Ops:
  6.5 691.0 %all-gather.2.cloned.1.call-start = ((), (), s32[]{:S(2)}) async-start(), calls=%async_computation.3 | async-start | bytes 37748736 | tf_op jit(solution)/shard_map/all_gather | solution.py:25
  224.6 496.0 %all-to-all-start.2 = ((f32[4,512,2048]{2,1,0:T(8,128)}), f32[4,512,2048]{2,1,0:T(8,128)}, u32[]{:S(2)}, u32[]{:S(2)}) async-start(f32[4,512,2048]{2,1,0:T(8,128)} %stack.10), calls=%async_computation.2 | async-start | bytes 33554432 | tf_op jit(solution)/shard_map/all_to_all | solution.py:9
Sparse Core Ops, SparseCore 0:
  12.2 685.3 all-gather.1
